TPU v7x, 32 devices: a whole 2x2x4 slice. The times are simulated.
32 devices in a mesh: grp: 4 (over y, x), dev: 8 (over z, core).
Axes of the slice: x: 2, y: 2, z: 4, core: 2. Of those that a mesh axis runs over, the one named last changes fastest.
Arguments:
- nz_user: int32 [4096, 128], P(('grp', 'dev')), may hold values from 0 to 8191
- nz_sub: int32 [4096, 128], P(('grp', 'dev')), may hold values from 0 to 2047
- nz_value: float32 [4096, 128], P(('grp', 'dev')), may hold values from -1 to 1
- tile_word: int32 [4096], P(('grp', 'dev')), may hold values from 0 to 2047, as said below
- word_owner: int32 [2048], replicated, may hold values from 0 to 2047, as said below
- user_factor: bfloat16 [64, 8192], P(None, 'dev'), may hold values from -6 to 6
- sub_factor: bfloat16 [64, 2048], P(None, 'dev'), may hold values from -6 to 6
Outputs:
- word_rows: float32 [64, 2048], P(None, ('grp', 'dev'))
Inputs may be any that keep to these rules, and one draw needn't show every extreme that they name: A permutation of the word indices: word w is summed into column word_owner[w] of word_rows. `tile_word`: tile i lies on device i // 128 (grp+dev order). On every device at most 2 tiles belong to words whose output column lies on any one other device, and on every device that bound is reached for some other device.
All inputs are finite; a program needn't handle non-finite values.
Results may differ from a plain program's by a relative error of at most 0.0003.
Values may be sent and summed in bfloat16 or wider, within the bound.
A program may use at most 64 MiB of HBM per device.

v0:
```python
import jax
import jax.numpy as jnp
from jax import lax
from jax.sharding import PartitionSpec as P

CAP = 2


def tile_sums(user_table, sub_table, nz_user, nz_sub, nz_value):
    tile_count, tile_width = nz_user.shape
    block_tiles = min(tile_count, 128)
    block_count = tile_count // block_tiles

    def one_block(block_args):
        users_block, subs_block, vals_block = block_args
        user_rows = jnp.take(user_table, users_block, axis=0).astype(jnp.float32)
        sub_rows = jnp.take(sub_table, subs_block, axis=0).astype(jnp.float32)
        return jnp.sum(user_rows * sub_rows * vals_block[:, :, None], axis=1)

    block_sums = lax.map(
        one_block,
        (
            nz_user.reshape(block_count, block_tiles, tile_width),
            nz_sub.reshape(block_count, block_tiles, tile_width),
            nz_value.reshape(block_count, block_tiles, tile_width),
        ),
    )
    return block_sums.reshape(tile_count, block_sums.shape[2])


def shards(nz_user, nz_sub, nz_value, tile_word, word_owner, user_factor, sub_factor):
    users_all, subs_all = (
        lax.all_gather(user_factor, "dev", axis=1, tiled=True),
        lax.all_gather(sub_factor, "dev", axis=1, tiled=True),
    )
    user_table = jnp.transpose(users_all)
    sub_table = jnp.transpose(subs_all)
    tile_rows = tile_sums(user_table, sub_table, nz_user, nz_sub, nz_value)
    tile_count, rank_width = tile_rows.shape
    grp_size = lax.axis_size("grp")
    dev_size = lax.axis_size("dev")
    devices_all = grp_size * dev_size
    words_total = word_owner.shape[0]
    words_local = words_total // devices_all
    out_rows = jnp.take(word_owner, tile_word)
    self_index = lax.axis_index("grp") * dev_size + lax.axis_index("dev")
    owner_dev = out_rows // words_local
    local_row = out_rows - owner_dev * words_local
    owned = owner_dev == self_index
    columns = jnp.arange(words_local, dtype=jnp.int32)
    own_table = (owned[:, None] & (local_row[:, None] == columns[None, :])).astype(jnp.float32)
    own_part = jnp.einsum("tr,tk->rk", tile_rows, own_table, precision=lax.Precision.HIGHEST)
    peer_ids = jnp.arange(devices_all, dtype=jnp.int32)
    outgoing = (jnp.logical_not(owned)[:, None] & (owner_dev[:, None] == peer_ids[None, :])).astype(
        jnp.float32
    )
    tile_ids = jnp.arange(tile_count, dtype=jnp.int32)
    earlier_table = (tile_ids[:, None] > tile_ids[None, :]).astype(jnp.float32)
    earlier = jnp.dot(
        earlier_table, outgoing, precision=lax.Precision.HIGHEST, preferred_element_type=jnp.float32
    )
    position = jnp.sum(earlier * outgoing, axis=1).astype(jnp.int32)
    send_slot = jnp.where(owned, devices_all * CAP, owner_dev * CAP + position)
    slot_ids = jnp.arange(devices_all * CAP, dtype=jnp.int32)
    slot_table = (send_slot[:, None] == slot_ids[None, :]).astype(jnp.float32)
    send_rows = jnp.einsum("ts,tr->sr", slot_table, tile_rows, precision=lax.Precision.HIGHEST)
    filled = jnp.sum(slot_table, axis=0)
    send_ids = (
        jnp.dot(
            local_row.astype(jnp.float32),
            slot_table,
            precision=lax.Precision.HIGHEST,
            preferred_element_type=jnp.float32,
        )
        + filled
        - 1.0
    )
    send_rows = send_rows.reshape(grp_size, dev_size, CAP * rank_width)
    send_ids = send_ids.reshape(grp_size, dev_size, CAP)
    got_rows, got_ids = (
        lax.all_to_all(
            lax.all_to_all(send_rows, "grp", split_axis=0, concat_axis=0, tiled=True),
            "dev",
            split_axis=1,
            concat_axis=1,
            tiled=True,
        ),
        lax.all_to_all(
            lax.all_to_all(send_ids, "grp", split_axis=0, concat_axis=0, tiled=True),
            "dev",
            split_axis=1,
            concat_axis=1,
            tiled=True,
        ),
    )
    got_rows = got_rows.reshape(devices_all * CAP, rank_width)
    got_ids = got_ids.reshape(devices_all * CAP).astype(jnp.int32)
    got_table = (got_ids[:, None] == columns[None, :]).astype(jnp.float32)
    far_part = jnp.einsum("sr,sk->rk", got_rows, got_table, precision=lax.Precision.HIGHEST)
    return own_part + far_part


def solution(mesh):
    return jax.shard_map(
        shards,
        mesh=mesh,
        in_specs=(
            P(("grp", "dev"), None),
            P(("grp", "dev"), None),
            P(("grp", "dev"), None),
            P(("grp", "dev")),
            P(),
            P(None, "dev"),
            P(None, "dev"),
        ),
        out_specs=P(None, ("grp", "dev")),
        check_vma=False,
    )
```

profile of v0, /device:TPU:0, one launch (start us, length us, event | category | flops | bytes accessed | tf_op | source)
XLA Modules:
  0.0 198.2 jit_solution(13226460569784429638)
XLA Ops:
  6.5 1.8 copy.39
  8.3 0.7 compare_select_fusion.2
  9.0 1.1 gather_fusion.2
  10.2 0.7 fusion.16
  11.0 0.7 add_select_fusion
  12.1 0.7 copy.43
  12.7 5.2 %all-to-all-start.2 = ((f32[4,8,2]{1,2,0:T(2,128)}), f32[4,8,2]{1,2,0:T(2,128)S(1)}, u32[]{:S(2)}, u32[]{:S(2)}) async-start(f32[4,8,2]{1,2,0:T(2,128)} %copy.43), calls=%async_computation.2 | async-start | bytes 8192 | tf_op jit(solution)/shard_map/all_to_all | solution.py:89
  17.9 0.9 copy.40
  18.8 0.9 compare_and_fusion
  19.7 0.9 bitcast_clamp_fusion.1
  20.6 0.9 bitcast_clamp_fusion
  21.5 17.7 %all_gather.7 = bf16[64,2048]{0,1:T(8,128)(2,1)S(1)} all-gather(bf16[64,256]{0,1:T(8,128)(2,1)S(1)} %copy.40), channel_id=1, replica_groups=mesh['grp'=4,'dev'=8] {'dev'}, dimensions={1}, use_global_device_ids=true | all-gather | bytes 294912 | tf_op jit(solution)/shard_map/all_gather | solution.py:34
  39.1 57.4 %gather_fusion.1 = bf16[16384,64]{1,0:T(8,128)(2,1)} fusion(bf16[2048,64]{1,0:T(8,128)(2,1)S(1)} %bitcast.22, s32[16384]{0:T(1024)S(1)} %bitcast_clamp_fusion), kind=kCustom, calls=%fused_computation.1 | custom fusion | bytes 4259840 | tf_op jit(solution)/shard_map/while/body/eval_jaxpr/jit(_take)/gather | solution.py:17
  96.5 0.7 copy.44
  97.2 4.8 %all-to-all-start.3 = ((f32[4,8,2]{0,2,1:T(2,128)}), f32[4,8,2]{0,2,1:T(2,128)S(1)}, u32[]{:S(2)}, u32[]{:S(2)}) async-start(f32[4,8,2]{0,2,1:T(2,128)} %copy.44), calls=%async_computation.3 | async-start | bytes 16384 | tf_op jit(solution)/shard_map/all_to_all | solution.py:88
  102.0 56.8 %gather_fusion = bf16[16384,64]{1,0:T(8,128)(2,1)} fusion(bf16[8192,64]{1,0:T(8,128)(2,1)} %bitcast.23, s32[16384]{0:T(1024)S(1)} %bitcast_clamp_fusion.1), kind=kCustom, calls=%fused_computation | custom fusion | bytes 4259840 | tf_op jit(solution)/shard_map/while/body/eval_jaxpr/jit(_take)/gather | solution.py:16
  158.8 10.6 %multiply_reduce_fusion = f32[128,64]{1,0:T(8,128)S(1)} fusion(f32[128,128]{1,0:T(8,128)S(1)} %copy-done.1, pred[128,128]{1,0:T(8,128)(4,1)S(1)} %get-tuple-element.30, pred[128,128]{1,0:T(8,128)(4,1)S(1)} %get-tuple-element.32, bf16[16384,64]{1,0:T(8,128)(2,1)} %gather_fusion.1, bf16[16384,64]{1,0:T(8,128)(2,1)} %gather_fusion), kind=kLoop, calls=%fused_computation.3 | loop fusion | flops 7331840 | bytes 4325376 | tf_op jit(solution)/shard_map/while/body/eval_jaxpr/reduce_sum | solution.py:18
  169.6 0.7 reshape.79
  170.3 4.1 %all-to-all-start = ((f32[4,8,128]{2,1,0:T(8,128)}), f32[4,8,128]{2,1,0:T(8,128)S(1)}, u32[]{:S(2)}, u32[]{:S(2)}) async-start(f32[4,8,128]{2,1,0:T(8,128)} %reshape.79), calls=%async_computation | async-start | bytes 32768 | tf_op jit(solution)/shard_map/all_to_all | solution.py:82
  174.7 4.4 %all-to-all-done = f32[4,8,128]{2,1,0:T(8,128)S(1)} async-done(((f32[4,8,128]{2,1,0:T(8,128)}), f32[4,8,128]{2,1,0:T(8,128)S(1)}, u32[]{:S(2)}, u32[]{:S(2)}) %all-to-all-start) | async-done | bytes 16416 | tf_op jit(solution)/shard_map/all_to_all | solution.py:82
  179.1 0.6 copy.41
  179.7 5.1 %all-to-all-start.1 = ((f32[4,8,128]{2,0,1:T(4,128)}), f32[4,8,128]{2,0,1:T(4,128)S(1)}, u32[]{:S(2)}, u32[]{:S(2)}) async-start(f32[4,8,128]{2,0,1:T(4,128)} %copy.41), calls=%async_computation.1 | async-start | bytes 32768 | tf_op jit(solution)/shard_map/all_to_all | solution.py:81
  185.1 5.4 %all-to-all-done.1 = f32[4,8,128]{2,0,1:T(4,128)S(1)} async-done(((f32[4,8,128]{2,0,1:T(4,128)}), f32[4,8,128]{2,0,1:T(4,128)S(1)}, u32[]{:S(2)}, u32[]{:S(2)}) %all-to-all-start.1) | async-done | bytes 16416 | tf_op jit(solution)/shard_map/all_to_all | solution.py:81
  190.5 0.9 convolution_add_fusion
  (22 shorter events, 1.4 us)
Async XLA Ops:
  6.5 2.5 %copy-start = (s32[2048]{0:T(1024)S(1)}, s32[2048]{0:T(1024)}, u32[]{:S(2)}) copy-start(s32[2048]{0:T(1024)} %param.11) | copy-start | bytes 24580
  6.5 95.5 %all-gather.2.cloned.1.call-start = ((), (), s32[]{:S(2)}) async-start(), calls=%async_computation.4 | async-start | bytes 2359296 | tf_op jit(solution)/shard_map/all_gather | solution.py:33
  12.7 83.8 %all-to-all-start.2 = ((f32[4,8,2]{1,2,0:T(2,128)}), f32[4,8,2]{1,2,0:T(2,128)S(1)}, u32[]{:S(2)}, u32[]{:S(2)}) async-start(f32[4,8,2]{1,2,0:T(2,128)} %copy.43), calls=%async_computation.2 | async-start | bytes 8192 | tf_op jit(solution)/shard_map/all_to_all | solution.py:89
  97.2 73.1 %all-to-all-start.3 = ((f32[4,8,2]{0,2,1:T(2,128)}), f32[4,8,2]{0,2,1:T(2,128)S(1)}, u32[]{:S(2)}, u32[]{:S(2)}) async-start(f32[4,8,2]{0,2,1:T(2,128)} %copy.44), calls=%async_computation.3 | async-start | bytes 16384 | tf_op jit(solution)/shard_map/all_to_all | solution.py:88
  102.0 56.8 %copy-start.1 = (f32[128,128]{1,0:T(8,128)S(1)}, f32[128,128]{1,0:T(8,128)}, u32[]{:S(2)}) copy-start(f32[128,128]{1,0:T(8,128)} %param.9) | copy-start | bytes 196612
  170.3 8.8 %all-to-all-start = ((f32[4,8,128]{2,1,0:T(8,128)}), f32[4,8,128]{2,1,0:T(8,128)S(1)}, u32[]{:S(2)}, u32[]{:S(2)}) async-start(f32[4,8,128]{2,1,0:T(8,128)} %reshape.79), calls=%async_computation | async-start | bytes 32768 | tf_op jit(solution)/shard_map/all_to_all | solution.py:82
  179.7 10.7 %all-to-all-start.1 = ((f32[4,8,128]{2,0,1:T(4,128)}), f32[4,8,128]{2,0,1:T(4,128)S(1)}, u32[]{:S(2)}, u32[]{:S(2)}) async-start(f32[4,8,128]{2,0,1:T(4,128)} %copy.41), calls=%async_computation.1 | async-start | bytes 32768 | tf_op jit(solution)/shard_map/all_to_all | solution.py:81
Sparse Core Ops, SparseCore 0:
  8.9 36.0 all-gather.1
where the time goes:
time: 199 us; the launch traced here: 198 us
  local copies, waits for them, and re-layouts  121 us (61%)
  starting transfers between devices  19.2 us (10%)
  blocking collectives  17.7 us (9%)
  other arithmetic  15.4 us (8%)
  between operations  13.5 us (7%)
  waiting for transfers between devices  9.81 us (5%)
    gather x1, local copies, waits for them, and re-layouts, one_block(): sub_rows = jnp.take(sub_table, subs_block, axis=0).astype(jnp.float32)  57.4 us
    gather x1, local copies, waits for them, and re-layouts, one_block(): user_rows = jnp.take(user_table, users_block, axis=0).astype(jnp.float32)  56.8 us
    all_gather x1, blocking collectives, shards(): lax.all_gather(sub_factor, 'dev', axis=1, tiled=True)  17.7 us
    reduce_sum x1, other arithmetic, one_block(): return jnp.sum(user_rows * sub_rows * vals_block[:, :, None], axis=1)  10.6 us
    all_to_all x1, waiting for transfers between devices, shards(): lax.all_to_all(lax.all_to_all(send_rows, 'grp', split_axis=0, concat_axis...  5.38 us
    all_to_all x1, starting transfers between devices, shards(): lax.all_to_all(send_ids, 'grp', split_axis=0, concat_axis=0, tiled=True)  5.19 us
    all_to_all x1, starting transfers between devices, shards(): lax.all_to_all(lax.all_to_all(send_rows, 'grp', split_axis=0, concat_axis...  5.08 us
    all_to_all x1, starting transfers between devices, shards(): lax.all_to_all(lax.all_to_all(send_ids, 'grp', split_axis=0, concat_axis=...  4.77 us
  transfers between devices with their start and end apart: 5, of which 2 were waited for; matrix products, arithmetic and copies ran while one was open for 68% of the time, Pallas kernels for 0%

commit v1 on v0

--- a/solution.py
+++ b/solution.py
@@ -77,6 +77,14 @@
     )
     send_rows = send_rows.reshape(grp_size, dev_size, CAP * rank_width)
     send_ids = send_ids.reshape(grp_size, dev_size, CAP)
+
+    def _end_layers_all(base_x, in_dim, dim_at):
+        now = lax.axis_size("dev")
+        t1 = jnp.split(base_x, now, axis=in_dim)
+        aux = jnp.stack(t1)
+        s_next = lax.all_to_all(aux, "dev", 0, 0)
+        return jnp.concatenate(s_next, axis=dim_at)
+
     got_rows, got_ids = (
         lax.all_to_all(
             lax.all_to_all(send_rows, "grp", split_axis=0, concat_axis=0, tiled=True),
@@ -85,12 +93,8 @@
             concat_axis=1,
             tiled=True,
         ),
-        lax.all_to_all(
-            lax.all_to_all(send_ids, "grp", split_axis=0, concat_axis=0, tiled=True),
-            "dev",
-            split_axis=1,
-            concat_axis=1,
-            tiled=True,
+        _end_layers_all(
+            lax.all_to_all(send_ids, "grp", split_axis=0, concat_axis=0, tiled=True), 1, 1
         ),
     )
     got_rows = got_rows.reshape(devices_all * CAP, rank_width)

time: 199 us -> 204 us (1.025)
  local copies, waits for them, and re-layouts: 121 us -> 127 us
    unnamed x6 -> x13, local copies, waits for them, and re-layouts: 2.64 us -> 6.49 us
where the time goes in v1:
time: 204 us; the launch traced here: 203 us
  local copies, waits for them, and re-layouts  127 us (62%)
  starting transfers between devices  19.3 us (9%)
  blocking collectives  16.7 us (8%)
  other arithmetic  15.4 us (8%)
  between operations  13.5 us (7%)
  waiting for transfers between devices  9.87 us (5%)
    gather x1, local copies, waits for them, and re-layouts, one_block(): sub_rows = jnp.take(sub_table, subs_block, axis=0).astype(jnp.float32)  57.8 us
    gather x1, local copies, waits for them, and re-layouts, one_block(): user_rows = jnp.take(user_table, users_block, axis=0).astype(jnp.float32)  57.3 us
    all_gather x1, blocking collectives, shards(): lax.all_gather(sub_factor, 'dev', axis=1, tiled=True)  16.7 us
    reduce_sum x1, other arithmetic, one_block(): return jnp.sum(user_rows * sub_rows * vals_block[:, :, None], axis=1)  10.6 us
    unnamed x13, local copies, waits for them, and re-layouts  6.49 us
    all_to_all x1, waiting for transfers between devices, shards(): lax.all_to_all(lax.all_to_all(send_rows, 'grp', split_axis=0, concat_axis...  5.38 us
    all_to_all x1, starting transfers between devices, shards(): lax.all_to_all(send_ids, 'grp', split_axis=0, concat_axis=0, tiled=True)  5.19 us
    all_to_all x1, starting transfers between devices, shards(): lax.all_to_all(lax.all_to_all(send_rows, 'grp', split_axis=0, concat_axis...  5.07 us
  transfers between devices with their start and end apart: 5, of which 2 were waited for; matrix products, arithmetic and copies ran while one was open for 68% of the time, Pallas kernels for 0%

profile of v1, /device:TPU:0, one launch (start us, length us, event | category | flops | bytes accessed | tf_op | source)
XLA Modules:
  0.0 203.0 jit_solution(2702232803094259269)
XLA Ops:
  6.5 0.7 compare_select_fusion.2
  7.2 1.1 gather_fusion.2
  8.4 0.7 fusion.16
  9.2 0.7 add_select_fusion
  10.3 0.7 copy.75
  11.0 5.2 %all-to-all-start.2 = ((f32[4,8,2]{1,2,0:T(2,128)}), f32[4,8,2]{1,2,0:T(2,128)S(1)}, u32[]{:S(2)}, u32[]{:S(2)}) async-start(f32[4,8,2]{1,2,0:T(2,128)} %copy.75), calls=%async_computation.2 | async-start | bytes 8192 | tf_op jit(solution)/shard_map/all_to_all | solution.py:97
  16.2 1.7 copy.71
  17.9 0.9 bitcast_clamp_fusion.1
  18.8 0.9 compare_and_fusion
  19.7 0.9 bitcast_clamp_fusion
  20.6 0.9 copy.72
  21.5 16.7 %all_gather.7 = bf16[64,2048]{0,1:T(8,128)(2,1)S(1)} all-gather(bf16[64,256]{0,1:T(8,128)(2,1)S(1)} %copy.72), channel_id=1, replica_groups=mesh['grp'=4,'dev'=8] {'dev'}, dimensions={1}, use_global_device_ids=true | all-gather | bytes 294912 | tf_op jit(solution)/shard_map/all_gather | solution.py:34
  38.2 57.8 %gather_fusion.1 = bf16[16384,64]{1,0:T(8,128)(2,1)} fusion(bf16[2048,64]{1,0:T(8,128)(2,1)S(1)} %bitcast.44, s32[16384]{0:T(1024)S(1)} %bitcast_clamp_fusion), kind=kCustom, calls=%fused_computation.1 | custom fusion | bytes 4259840 | tf_op jit(solution)/shard_map/while/body/eval_jaxpr/jit(_take)/gather | solution.py:17
  100.7 0.6 constant_dynamic-update-slice_fusion
  101.3 4.9 %all-to-all-start.3 = ((f32[8,4,1,2]{1,3,2,0:T(2,128)}), f32[8,4,1,2]{1,3,2,0:T(2,128)S(1)}, u32[]{:S(2)}, u32[]{:S(2)}) async-start(f32[8,4,1,2]{1,3,2,0:T(2,128)} %constant_dynamic-update-slice_fusion), calls=%async_computation.3 | async-start | bytes 16384 | tf_op jit(solution)/shard_map/all_to_all | solution.py:85
  106.3 57.3 %gather_fusion = bf16[16384,64]{1,0:T(8,128)(2,1)} fusion(bf16[8192,64]{1,0:T(8,128)(2,1)} %bitcast.45, s32[16384]{0:T(1024)S(1)} %bitcast_clamp_fusion.1), kind=kCustom, calls=%fused_computation | custom fusion | bytes 4259840 | tf_op jit(solution)/shard_map/while/body/eval_jaxpr/jit(_take)/gather | solution.py:16
  163.6 10.6 %multiply_reduce_fusion = f32[128,64]{1,0:T(8,128)S(1)} fusion(f32[128,128]{1,0:T(8,128)S(1)} %copy-done.1, pred[128,128]{1,0:T(8,128)(4,1)S(1)} %get-tuple-element.39, pred[128,128]{1,0:T(8,128)(4,1)S(1)} %get-tuple-element.40, bf16[16384,64]{1,0:T(8,128)(2,1)} %gather_fusion.1, bf16[16384,64]{1,0:T(8,128)(2,1)} %gather_fusion), kind=kLoop, calls=%fused_computation.3 | loop fusion | flops 7331840 | bytes 4325376 | tf_op jit(solution)/shard_map/while/body/eval_jaxpr/reduce_sum | solution.py:18
  174.3 0.7 reshape.79
  175.0 4.1 %all-to-all-start = ((f32[4,8,128]{2,1,0:T(8,128)}), f32[4,8,128]{2,1,0:T(8,128)S(1)}, u32[]{:S(2)}, u32[]{:S(2)}) async-start(f32[4,8,128]{2,1,0:T(8,128)} %reshape.79), calls=%async_computation | async-start | bytes 32768 | tf_op jit(solution)/shard_map/all_to_all | solution.py:90
  179.4 4.5 %all-to-all-done = f32[4,8,128]{2,1,0:T(8,128)S(1)} async-done(((f32[4,8,128]{2,1,0:T(8,128)}), f32[4,8,128]{2,1,0:T(8,128)S(1)}, u32[]{:S(2)}, u32[]{:S(2)}) %all-to-all-start) | async-done | bytes 16416 | tf_op jit(solution)/shard_map/all_to_all | solution.py:90
  183.9 0.6 copy.73
  184.5 5.1 %all-to-all-start.1 = ((f32[4,8,128]{2,0,1:T(4,128)}), f32[4,8,128]{2,0,1:T(4,128)S(1)}, u32[]{:S(2)}, u32[]{:S(2)}) async-start(f32[4,8,128]{2,0,1:T(4,128)} %copy.73), calls=%async_computation.1 | async-start | bytes 32768 | tf_op jit(solution)/shard_map/all_to_all | solution.py:89
  189.8 5.4 %all-to-all-done.1 = f32[4,8,128]{2,0,1:T(4,128)S(1)} async-done(((f32[4,8,128]{2,0,1:T(4,128)}), f32[4,8,128]{2,0,1:T(4,128)S(1)}, u32[]{:S(2)}, u32[]{:S(2)}) %all-to-all-start.1) | async-done | bytes 16416 | tf_op jit(solution)/shard_map/all_to_all | solution.py:89
  195.3 0.9 convolution_add_fusion
  (37 shorter events, 6.1 us)
Async XLA Ops:
  6.5 0.7 copy-start
  11.0 85.0 %all-to-all-start.2 = ((f32[4,8,2]{1,2,0:T(2,128)}), f32[4,8,2]{1,2,0:T(2,128)S(1)}, u32[]{:S(2)}, u32[]{:S(2)}) async-start(f32[4,8,2]{1,2,0:T(2,128)} %copy.75), calls=%async_computation.2 | async-start | bytes 8192 | tf_op jit(solution)/shard_map/all_to_all | solution.py:97
  16.2 90.1 %all-gather.2.cloned.1.call-start = ((), (), s32[]{:S(2)}) async-start(), calls=%async_computation.4 | async-start | bytes 2359296 | tf_op jit(solution)/shard_map/all_gather | solution.py:33
  101.3 73.7 %all-to-all-start.3 = ((f32[8,4,1,2]{1,3,2,0:T(2,128)}), f32[8,4,1,2]{1,3,2,0:T(2,128)S(1)}, u32[]{:S(2)}, u32[]{:S(2)}) async-start(f32[8,4,1,2]{1,3,2,0:T(2,128)} %constant_dynamic-update-slice_fusion), calls=%async_computation.3 | async-start | bytes 16384 | tf_op jit(solution)/shard_map/all_to_all | solution.py:85
  106.2 57.3 %copy-start.1 = (f32[128,128]{1,0:T(8,128)S(1)}, f32[128,128]{1,0:T(8,128)}, u32[]{:S(2)}) copy-start(f32[128,128]{1,0:T(8,128)} %param.9) | copy-start | bytes 196612
  175.0 8.8 %all-to-all-start = ((f32[4,8,128]{2,1,0:T(8,128)}), f32[4,8,128]{2,1,0:T(8,128)S(1)}, u32[]{:S(2)}, u32[]{:S(2)}) async-start(f32[4,8,128]{2,1,0:T(8,128)} %reshape.79), calls=%async_computation | async-start | bytes 32768 | tf_op jit(solution)/shard_map/all_to_all | solution.py:90
  184.5 10.7 %all-to-all-start.1 = ((f32[4,8,128]{2,0,1:T(4,128)}), f32[4,8,128]{2,0,1:T(4,128)S(1)}, u32[]{:S(2)}, u32[]{:S(2)}) async-start(f32[4,8,128]{2,0,1:T(4,128)} %copy.73), calls=%async_computation.1 | async-start | bytes 32768 | tf_op jit(solution)/shard_map/all_to_all | solution.py:89
Sparse Core Ops, SparseCore 0:
  18.6 32.7 all-gather.1
